TPU v7x, 32 devices: a whole 2x2x4 slice. The times are simulated.
32 devices in a mesh: cls: 8 (over z, y), row: 4 (over x, core).
Axes of the slice: x: 2, y: 2, z: 4, core: 2. Of those that a mesh axis runs over, the one named last changes fastest.
Arguments:
- embeddings: float32 [1024, 1024], P('row'), may hold values from -6 to 6
- weights: float32 [1024, 81920], P(('cls', 'row')), may hold values from -4 to 4
- labels: int32 [1024], replicated, may hold values from 0 to 81919, as said below
Outputs:
- weight_update: float32 [1024, 81920], P(None, ('cls', 'row'))
- losses: float32 [2, 1024], replicated
Inputs may be any that keep to these rules, and one draw needn't show every extreme that they name: labels take at most 512 distinct values, at most one in each aligned run of 160 classes; rows may share a label.
All inputs are finite; a program needn't handle non-finite values.
Results may differ from a plain program's by a relative error of at most 0.012.
The roundings to bfloat16 on the way count: a program that leaves them out, or rounds other values in their place, can miss the bound.
Values may be sent and summed in bfloat16 or wider, within the bound.
A program may use at most 128 MiB of HBM per device.

v0:
```python
import functools

import jax
import jax.numpy as jnp
from jax import lax
from jax.experimental import pallas as pl
from jax.experimental.pallas import tpu as pltpu
from jax.sharding import PartitionSpec as P

STEPS = 2


learn_rate = 2.0

MESH = pl.DeviceIdType.MESH
LANES = 128
ROW_TILE = 256
SUB = 32


def exchange_kernel(
    cls_n,
    row_n,
    rate,
    emb_ref,
    weights_ref,
    labels_ref,
    total_ref,
    turned_ref,
    losses_ref,
    stage,
    outgoing,
    incoming,
    label_lanes,
    logits,
    gram,
    examples,
    emb_bf,
    peak_lanes,
    sum_lanes,
    pick_lanes,
    norm_lanes,
    row_send,
    row_recv,
    cls_send,
    cls_recv,
    load_sem,
    out_sem,
    in_sem,
    emb_out,
    emb_in,
    row_out,
    row_in,
    cls_out,
    cls_in,
):
    n = cls_n * row_n
    my_cls, my_row = lax.axis_index("cls"), lax.axis_index("row")
    me = my_cls * row_n + my_row
    chunks, rows, width = logits.shape
    features = outgoing.shape[2]
    class_count = chunks * width
    shard_rows = emb_ref.shape[0]
    tiles = rows // ROW_TILE
    groups = width // LANES
    slabs = rows // LANES

    def place(p):
        return (lax.div(p, row_n), lax.rem(p, row_n))

    def load(chunk, slot):
        @pl.loop(0, n)
        def _(p):
            start = pl.multiple_of(p * class_count + chunk * width, LANES)
            pltpu.make_async_copy(
                weights_ref.at[:, pl.ds(start, width)], stage.at[slot, p], load_sem.at[slot]
            ).start()

    load(0, 0)
    load(1, 1)

    barrier = pltpu.get_barrier_semaphore()

    @pl.loop(1, n)
    def _(k):
        pl.semaphore_signal(
            barrier, inc=1, device_id=place(lax.rem(me + k, n)), device_id_type=MESH
        )

    emb_bf[...] = emb_ref[...].astype(jnp.bfloat16)
    mine = pl.ds(pl.multiple_of(my_row * shard_rows, shard_rows), shard_rows)
    examples[mine, :] = emb_bf[...]
    pl.semaphore_wait(barrier, n - 1)

    @pl.loop(0, chunks)
    def _(c):
        slot = lax.rem(c, 2)
        pltpu.make_async_copy(stage.at[slot], stage.at[slot], load_sem.at[slot]).wait()
        spot = pl.ds(pl.multiple_of(me * features, features), features)

        def send(j):
            p = lax.rem(me + j + n // 2, n)
            outgoing[c, p] = stage[slot, p].astype(jnp.bfloat16)
            pltpu.make_async_remote_copy(
                src_ref=outgoing.at[c, p],
                dst_ref=incoming.at[c, spot],
                send_sem=out_sem.at[c],
                recv_sem=in_sem.at[c],
                device_id=place(p),
                device_id_type=MESH,
            ).start()

        pl.loop(0, n // 2)(send)
        incoming[c, spot] = stage[slot, me].astype(jnp.bfloat16)
        pl.loop(n // 2 + 1, n)(send)

        @pl.when(c == 0)
        def _():
            @pl.loop(1, row_n)
            def _(k):
                pltpu.make_async_remote_copy(
                    src_ref=emb_bf,
                    dst_ref=examples.at[mine],
                    send_sem=emb_out,
                    recv_sem=emb_in,
                    device_id=(my_cls, lax.rem(my_row + k, row_n)),
                    device_id_type=MESH,
                ).start()

        @pl.when(c + 2 < chunks)
        def _():
            load(c + 2, slot)

    peers = pl.ds(0, (row_n - 1) * shard_rows)
    pltpu.make_async_copy(examples.at[peers], examples.at[peers], emb_in).wait()

    @pl.loop(0, tiles)
    def _(i):
        here = pl.ds(pl.multiple_of(i * ROW_TILE, ROW_TILE), ROW_TILE)
        gram[here, :] = lax.dot_general(
            examples[here, :],
            examples[...],
            (((1,), (1,)), ((), ())),
            preferred_element_type=jnp.float32,
        ).astype(jnp.bfloat16)
        turned_ref[:, here] = examples[here, :].astype(jnp.float32).T.astype(jnp.bfloat16)

    for i in range(slabs):
        label_lanes[pl.ds(i * LANES, LANES), :] = (
            jnp.broadcast_to(labels_ref[i : i + 1, :], (LANES, LANES)).T - me * class_count
        )

    def reset():
        peak_lanes[...] = jnp.full_like(peak_lanes, -3.0e38)
        sum_lanes[...] = jnp.zeros_like(sum_lanes)
        pick_lanes[...] = jnp.zeros_like(pick_lanes)

    def hits(spot, c):
        shifted = label_lanes[spot, :] - c * width
        lane = lax.broadcasted_iota(jnp.int32, shifted.shape, 1)
        return [lane + q * LANES == shifted for q in range(groups)]

    def collect(c, spot, block):
        parts = [block[:, q * LANES : (q + 1) * LANES] for q in range(groups)]
        old = peak_lanes[spot, :]
        peak = functools.reduce(jnp.maximum, parts, old)
        total = sum_lanes[spot, :] * jnp.exp(old - peak)
        picked = pick_lanes[spot, :]
        for part, hit in zip(parts, hits(spot, c)):
            total = total + jnp.exp(part - peak)
            picked = picked + jnp.where(hit, part, 0.0)
        peak_lanes[spot, :] = peak
        sum_lanes[spot, :] = total
        pick_lanes[spot, :] = picked

    def share(t, send_buf, recv_buf, send_sem, recv_sem, count, mine_at, target):
        recv_buf[t, mine_at] = send_buf[t]

        @pl.loop(1, count)
        def _(k):
            pltpu.make_async_remote_copy(
                src_ref=send_buf.at[t],
                dst_ref=recv_buf.at[t, mine_at],
                send_sem=send_sem.at[t],
                recv_sem=recv_sem.at[t],
                device_id=target(k),
                device_id_type=MESH,
            ).start()

        every = pl.ds(0, count - 1)
        pltpu.make_async_copy(recv_buf.at[t, every], recv_buf.at[t, every], recv_sem.at[t]).wait()
        norms = recv_buf[t, :, :slabs, :]
        top = jnp.max(norms, axis=0)
        norm = top + jnp.log(jnp.sum(jnp.exp(norms - top[None]), axis=0))
        picked = jnp.sum(recv_buf[t, :, slabs:, :], axis=0)
        pltpu.make_async_copy(recv_buf.at[t, every], recv_buf.at[t, every], send_sem.at[t]).wait()
        return norm, picked

    def settle(t):
        for i in range(slabs):
            part = pl.ds(i * LANES, LANES)
            peaks = peak_lanes[part, :].T
            top = jnp.max(peaks, axis=0, keepdims=True)
            total = jnp.sum(sum_lanes[part, :].T * jnp.exp(peaks - top), axis=0, keepdims=True)
            row_send[t, i : i + 1, :] = top + jnp.log(total)
            row_send[t, slabs + i : slabs + i + 1, :] = jnp.sum(
                pick_lanes[part, :].T, axis=0, keepdims=True
            )
        norm, picked = share(
            t, row_send, row_recv, row_out, row_in, row_n, my_row,
            lambda k: (my_cls, lax.rem(my_row + k, row_n)),
        )
        cls_send[t, :slabs, :] = norm
        cls_send[t, slabs:, :] = picked
        norm, picked = share(
            t, cls_send, cls_recv, cls_out, cls_in, cls_n, my_cls,
            lambda k: (lax.rem(my_cls + k, cls_n), my_row),
        )
        loss = norm - picked
        for i in range(slabs):
            losses_ref[t : t + 1, i * LANES : (i + 1) * LANES] = loss[i : i + 1, :]
            norm_lanes[pl.ds(i * LANES, LANES), :] = jnp.broadcast_to(
                norm[i : i + 1, :], (LANES, LANES)
            ).T

    def residual(c, spot, earlier):
        norm = norm_lanes[spot, :]
        block = logits[c, spot, :]
        for q, hit in enumerate(hits(spot, c)):
            columns = slice(q * LANES, (q + 1) * LANES)
            value = jnp.exp(block[:, columns] - norm) - jnp.where(hit, 1.0, 0.0)
            if earlier:
                value = value + total_ref[c, spot, columns].astype(jnp.float32)
            total_ref[c, spot, columns] = value.astype(jnp.bfloat16)

    reset()

    @pl.loop(0, chunks)
    def _(c):
        arrived = pl.ds(0, (n - 1) * features)
        pltpu.make_async_copy(
            incoming.at[c, arrived], incoming.at[c, arrived], in_sem.at[c]
        ).wait()

        @pl.loop(0, tiles)
        def _(i):
            here = pl.ds(pl.multiple_of(i * ROW_TILE, ROW_TILE), ROW_TILE)
            logits[c, here, :] = jnp.dot(
                examples[here, :], incoming[c], preferred_element_type=jnp.float32
            )

            @pl.loop(0, ROW_TILE // SUB, unroll=2)
            def _(u):
                spot = pl.ds(pl.multiple_of(i * ROW_TILE + u * SUB, SUB), SUB)
                collect(c, spot, logits[c, spot, :])

    settle(0)
    reset()

    @pl.loop(0, rows // SUB, unroll=4)
    def _(u):
        residual(0, pl.ds(pl.multiple_of(u * SUB, SUB), SUB), False)

    for c in range(chunks):
        for i in range(tiles):
            here = pl.ds(i * ROW_TILE, ROW_TILE)
            change = jnp.dot(gram[here, :], total_ref[c], preferred_element_type=jnp.float32)
            if c + 1 < chunks:
                residual(c + 1, here, False)
            block = logits[c, here, :] - rate * change
            logits[c, here, :] = block
            collect(c, here, block)

    settle(1)

    @pl.loop(0, chunks)
    def _(c):
        @pl.loop(0, rows // SUB, unroll=4)
        def _(u):
            residual(c, pl.ds(pl.multiple_of(u * SUB, SUB), SUB), True)

    pltpu.make_async_copy(examples.at[peers], examples.at[peers], emb_out).wait()

    @pl.loop(0, chunks)
    def _(c):
        sent = pl.ds(0, n - 1)
        pltpu.make_async_copy(outgoing.at[c, sent], outgoing.at[c, sent], out_sem.at[c]).wait()


def update_kernel(rate, turned_ref, total_ref, out_ref):
    out_ref[...] = -rate * jnp.dot(
        turned_ref[...], total_ref[0], preferred_element_type=jnp.float32
    )


def fused(embeddings, weights, labels):
    cls_n, row_n = lax.axis_size("cls"), lax.axis_size("row")
    n = cls_n * row_n
    shard_rows, model_width = embeddings.shape
    rows = shard_rows * row_n
    features = weights.shape[0]
    class_count = weights.shape[1] // n
    width = max(w for w in (128, 256, 384, 512) if class_count % w == 0)
    chunks = class_count // width
    rate = learn_rate / rows
    slabs = rows // LANES
    vmem = pl.BlockSpec(memory_space=pltpu.VMEM)
    dma = pltpu.SemaphoreType.DMA
    total, turned, losses = pl.pallas_call(
        functools.partial(exchange_kernel, cls_n, row_n, rate),
        out_shape=(
            jax.ShapeDtypeStruct((chunks, rows, width), jnp.bfloat16),
            jax.ShapeDtypeStruct((model_width, rows), jnp.bfloat16),
            jax.ShapeDtypeStruct((STEPS, rows), jnp.float32),
        ),
        in_specs=[vmem, pl.BlockSpec(memory_space=pl.ANY), vmem],
        out_specs=(vmem, vmem, vmem),
        scratch_shapes=[
            pltpu.VMEM((2, n, features, width), jnp.float32),
            pltpu.VMEM((chunks, n, features, width), jnp.bfloat16),
            pltpu.VMEM((chunks, n * features, width), jnp.bfloat16),
            pltpu.VMEM((rows, LANES), jnp.int32),
            pltpu.VMEM((chunks, rows, width), jnp.float32),
            pltpu.VMEM((rows, rows), jnp.bfloat16),
            pltpu.VMEM((rows, model_width), jnp.bfloat16),
            pltpu.VMEM((shard_rows, model_width), jnp.bfloat16),
            pltpu.VMEM((rows, LANES), jnp.float32),
            pltpu.VMEM((rows, LANES), jnp.float32),
            pltpu.VMEM((rows, LANES), jnp.float32),
            pltpu.VMEM((rows, LANES), jnp.float32),
            pltpu.VMEM((STEPS, 2 * slabs, LANES), jnp.float32),
            pltpu.VMEM((STEPS, row_n, 2 * slabs, LANES), jnp.float32),
            pltpu.VMEM((STEPS, 2 * slabs, LANES), jnp.float32),
            pltpu.VMEM((STEPS, cls_n, 2 * slabs, LANES), jnp.float32),
            dma((2,)),
            dma((chunks,)),
            dma((chunks,)),
            dma,
            dma,
            dma((STEPS,)),
            dma((STEPS,)),
            dma((STEPS,)),
            dma((STEPS,)),
        ],
        compiler_params=pltpu.CompilerParams(
            collective_id=0, has_side_effects=True, vmem_limit_bytes=60 * 1024 * 1024
        ),
    )(embeddings, weights, labels.reshape(slabs, LANES))
    tall = model_width // 2
    update = pl.pallas_call(
        functools.partial(update_kernel, rate),
        grid=(chunks, 2),
        out_shape=jax.ShapeDtypeStruct((model_width, class_count), jnp.float32),
        in_specs=[
            pl.BlockSpec((tall, rows), lambda c, i: (i, 0)),
            pl.BlockSpec((1, rows, width), lambda c, i: (c, 0, 0)),
        ],
        out_specs=pl.BlockSpec((tall, width), lambda c, i: (i, c)),
        compiler_params=pltpu.CompilerParams(
            dimension_semantics=("arbitrary", "arbitrary"), vmem_limit_bytes=60 * 1024 * 1024
        ),
    )(turned, total)
    return update, losses


def shards(embeddings, weights, labels):
    if STEPS == 2 and weights.shape[0] % 16 == 0:
        return fused(embeddings, weights, labels)
    peer_count = lax.axis_size(("cls", "row"))
    examples = lax.all_gather(embeddings.astype(jnp.bfloat16), "row", axis=0, tiled=True)
    row_count = examples.shape[0]
    feature_rows = weights.shape[0]
    class_count = weights.shape[1] // peer_count
    offset = lax.axis_index(("cls", "row")) * class_count
    columns = lax.broadcasted_iota(jnp.int32, (1, class_count), 1) + offset
    label_hit = columns == labels[:, None]
    pieces = weights.astype(jnp.bfloat16).reshape(feature_rows, peer_count, class_count)
    block_weights = lax.all_to_all(
        pieces.transpose(1, 0, 2), ("cls", "row"), split_axis=0, concat_axis=0, tiled=True
    )
    flat_weights = block_weights.reshape(peer_count * feature_rows, class_count)
    first_logits = jnp.dot(examples, flat_weights, preferred_element_type=jnp.float32)
    rate = learn_rate / row_count
    gram = lax.dot_general(
        examples, examples, (((1,), (1,)), ((), ())), preferred_element_type=jnp.float32
    ).astype(jnp.bfloat16)
    total = None
    loss_rows = []
    for step_index in range(STEPS):
        logits = first_logits
        if step_index > 0:
            logits = logits - rate * jnp.dot(gram, total, preferred_element_type=jnp.float32)
        local_peak = jnp.max(logits, axis=1)
        local_total = jnp.sum(jnp.exp(logits - local_peak[:, None]), axis=1)
        local_picked = jnp.sum(jnp.where(label_hit, logits, 0.0), axis=1)
        stats = lax.all_gather(
            jnp.stack([local_peak, local_total, local_picked]), ("cls", "row"), axis=0
        )
        row_peak = jnp.max(stats[:, 0], axis=0)
        row_total = jnp.sum(stats[:, 1] * jnp.exp(stats[:, 0] - row_peak[None, :]), axis=0)
        picked = jnp.sum(stats[:, 2], axis=0)
        log_norm = row_peak + jnp.log(row_total)
        loss_rows.append(log_norm - picked)
        onehot = jnp.where(label_hit, 1.0, 0.0)
        residual = jnp.exp(logits - log_norm[:, None]) - onehot
        if total is not None:
            residual = residual + total.astype(jnp.float32)
        total = residual.astype(jnp.bfloat16)
    update = lax.dot_general(
        examples, total, (((0,), (0,)), ((), ())), preferred_element_type=jnp.float32
    )
    return (-rate * update, jnp.stack(loss_rows))


def solution(mesh):
    placed = (P("row", None), P(("cls", "row"), None), P())
    return jax.shard_map(
        shards,
        mesh=mesh,
        in_specs=placed,
        out_specs=(P(None, ("cls", "row")), P()),
        check_vma=False,
    )
```

profile of v0, /device:TPU:0, one launch (start us, length us, event | category | flops | bytes accessed | tf_op | source)
XLA Modules:
  0.0 175.1 jit_solution(15722346554042825376)
XLA Ops:
  0.6 157.8 %shard_map.50 = (bf16[5,1024,512]{2,1,0:T(8,128)(2,1)}, bf16[1024,1024]{1,0:T(8,128)(2,1)}, f32[2,1024]{1,0:T(2,128)}) custom-call(f32[256,1024]{1,0:T(8,128)} %emb_ref.1, f32[32,81920]{1,0:T(8,128)} %weights_ref.1, s32[8,128]{1,0:T(8,128)} %bitcast.1), custom_call_target="tpu_custom_call" | custom-call | tf_op jit(solution)/shard_map/pallas_call | solution.py:309
  158.4 0.0 copy-start
  158.4 16.1 %shard_map.51 = f32[1024,2560]{1,0:T(8,128)} custom-call(bf16[1024,1024]{1,0:T(8,128)(2,1)} %get-tuple-element.5.turned_ref, bf16[5,1024,512]{2,1,0:T(8,128)(2,1)} %get-tuple-element.6.total_ref), custom_call_target="tpu_custom_call" | custom-call | tf_op jit(solution)/shard_map/pallas_call | solution.py:350
  174.5 0.0 copy-done
  174.5 0.6 copy.6
Async XLA Ops:
  158.4 16.1 %copy-start = (f32[2,1024]{1,0:T(2,128)S(1)}, f32[2,1024]{1,0:T(2,128)}, u32[]{:S(2)}) copy-start(f32[2,1024]{1,0:T(2,128)} %get-tuple-element.11) | copy-start | bytes 24580
where the time goes:
time: 175 us
  Pallas kernels  174 us (99%)
    pallas_call x1, Pallas kernels, fused(): pl.pallas_call(functools.partial(exchange_kernel, cls_n, row_n, rate), ou...  158 us
    pallas_call x1, Pallas kernels, fused(): pl.pallas_call(functools.partial(update_kernel, rate), grid=(chunks, 2),...  16.1 us

commit v1 on v0

v1 whole, which is shorter than its diff:
```python
import functools

import jax
import jax.numpy as jnp
from jax import lax
from jax.experimental import pallas as pl
from jax.experimental.pallas import tpu as pltpu
from jax.sharding import PartitionSpec as P

STEPS = 2


learn_rate = 2.0

MESH = pl.DeviceIdType.MESH
LANES = 128
ROW_TILE = 256
SUB = 32
HALVES = 2
LOG2E = 1.4426950408889634
LN2 = 0.6931471805599453
KERNEL_VMEM = 40 * 1024 * 1024
UPDATE_VMEM = 24 * 1024 * 1024


def exchange_kernel(
    cls_n,
    row_n,
    rate,
    emb_hbm,
    weights_ref,
    labels_hbm,
    total_ref,
    turned_ref,
    losses_ref,
    stage,
    outgoing,
    incoming,
    label_lanes,
    logits,
    gram,
    examples,
    emb_ref,
    emb_bf,
    labels_ref,
    peak_lanes,
    sum_lanes,
    pick_lanes,
    norm_lanes,
    hit_lanes,
    first_send,
    first_recv,
    later_send,
    later_recv,
    load_sem,
    small_sem,
    out_sem,
    in_sem,
    emb_out,
    emb_in,
    first_out,
    first_in,
    later_out,
    later_in,
):
    n = cls_n * row_n
    my_cls, my_row = lax.axis_index("cls"), lax.axis_index("row")
    me = my_cls * row_n + my_row
    chunks, rows, width = logits.shape
    pieces, _, features, narrow = outgoing.shape
    per = width // narrow
    class_count = chunks * width
    shard_rows = emb_ref.shape[0]
    tiles = rows // ROW_TILE
    groups = width // LANES
    slabs = rows // LANES

    def place(p):
        return (lax.div(p, row_n), lax.rem(p, row_n))

    barrier = pltpu.get_barrier_semaphore()

    @pl.loop(1, n)
    def _(k):
        pl.semaphore_signal(
            barrier, inc=1, device_id=place(lax.rem(me + k, n)), device_id_type=MESH
        )

    def load(piece, slot):
        @pl.loop(0, n)
        def _(p):
            start = pl.multiple_of(p * class_count + piece * narrow, LANES)
            pltpu.make_async_copy(
                weights_ref.at[:, pl.ds(start, narrow)], stage.at[slot, p], load_sem.at[slot]
            ).start()

    load(0, 0)
    emb_copy = pltpu.make_async_copy(emb_hbm, emb_ref, small_sem.at[0])
    emb_copy.start()
    labels_copy = pltpu.make_async_copy(labels_hbm, labels_ref, small_sem.at[1])
    labels_copy.start()
    load(1, 1)

    emb_copy.wait()
    emb_bf[...] = emb_ref[...].astype(jnp.bfloat16)
    mine = pl.ds(pl.multiple_of(my_row * shard_rows, shard_rows), shard_rows)
    examples[mine, :] = emb_bf[...]
    labels_copy.wait()
    pl.semaphore_wait(barrier, n - 1)

    @pl.loop(0, pieces)
    def _(c):
        slot = lax.rem(c, 2)
        pltpu.make_async_copy(stage.at[slot], stage.at[slot], load_sem.at[slot]).wait()
        spot = pl.ds(pl.multiple_of(me * features, features), features)

        def send(j):
            p = lax.rem(me + j + n // 2, n)
            outgoing[c, p] = stage[slot, p].astype(jnp.bfloat16)
            pltpu.make_async_remote_copy(
                src_ref=outgoing.at[c, p],
                dst_ref=incoming.at[c, spot],
                send_sem=out_sem.at[c],
                recv_sem=in_sem.at[c],
                device_id=place(p),
                device_id_type=MESH,
            ).start()

        pl.loop(0, n // 2)(send)
        incoming[c, spot] = stage[slot, me].astype(jnp.bfloat16)
        pl.loop(n // 2 + 1, n)(send)

        @pl.when(c == 0)
        def _():
            @pl.loop(1, row_n)
            def _(k):
                pltpu.make_async_remote_copy(
                    src_ref=emb_bf,
                    dst_ref=examples.at[mine],
                    send_sem=emb_out,
                    recv_sem=emb_in,
                    device_id=(my_cls, lax.rem(my_row + k, row_n)),
                    device_id_type=MESH,
                ).start()

        @pl.when(c + 2 < pieces)
        def _():
            load(c + 2, slot)

    for i in range(slabs):
        label_lanes[pl.ds(i * LANES, LANES), :] = (
            jnp.broadcast_to(labels_ref[i : i + 1, :], (LANES, LANES)).T - me * class_count
        )

    peers = pl.ds(0, (row_n - 1) * shard_rows)
    pltpu.make_async_copy(examples.at[peers], examples.at[peers], emb_in).wait()

    @pl.loop(0, tiles)
    def _(i):
        here = pl.ds(pl.multiple_of(i * ROW_TILE, ROW_TILE), ROW_TILE)
        product = lax.dot_general(
            examples[here, :],
            examples[...],
            (((1,), (1,)), ((), ())),
            preferred_element_type=jnp.float32,
        )
        gram[here, :] = (product * (rate * LOG2E)).astype(jnp.bfloat16)
        turned_ref[:, here] = examples[here, :].astype(jnp.float32).T.astype(jnp.bfloat16)

    def reset():
        peak_lanes[...] = jnp.full_like(peak_lanes, -3.0e38)
        sum_lanes[...] = jnp.zeros_like(sum_lanes)
        pick_lanes[...] = jnp.zeros_like(pick_lanes)

    def hits(spot, offset, count):
        shifted = label_lanes[spot, :] - offset
        lane = lax.broadcasted_iota(jnp.int32, shifted.shape, 1)
        return [lane + q * LANES == shifted for q in range(count)]

    def collect(spot, offset, block):
        count = block.shape[1] // LANES
        parts = [block[:, q * LANES : (q + 1) * LANES] for q in range(count)]
        old = peak_lanes[spot, :]
        peak = functools.reduce(jnp.maximum, parts, old)
        total = sum_lanes[spot, :] * jnp.exp2(old - peak)
        picked = pick_lanes[spot, :]
        for part, hit in zip(parts, hits(spot, offset, count)):
            total = total + jnp.exp2(part - peak)
            picked = jnp.where(hit, part, picked)
        peak_lanes[spot, :] = peak
        sum_lanes[spot, :] = total
        pick_lanes[spot, :] = picked

    def residual(c, spot, earlier):
        norm = norm_lanes[spot, :]
        at_label = hit_lanes[spot, :]
        for q, hit in enumerate(hits(spot, c * width, groups)):
            columns = slice(q * LANES, (q + 1) * LANES)
            part = logits[c, spot, columns]
            value = jnp.where(hit, at_label, jnp.exp2(part - norm)).astype(jnp.bfloat16)
            if earlier:
                value = value + total_ref[c, spot, columns]
            total_ref[c, spot, columns] = value

    def share(src, dst, send_sem, recv_sem):
        @pl.loop(1, n)
        def _(k):
            pltpu.make_async_remote_copy(
                src_ref=src,
                dst_ref=dst.at[me],
                send_sem=send_sem,
                recv_sem=recv_sem,
                device_id=place(lax.rem(me + k, n)),
                device_id_type=MESH,
            ).start()

    def publish(first, count, sent, landed, send_sem, recv_sem):
        for i in range(count):
            part = pl.ds((first + i) * LANES, LANES)
            peaks = peak_lanes[part, :].T
            top = jnp.max(peaks, axis=0, keepdims=True)
            total = jnp.sum(sum_lanes[part, :].T * jnp.exp2(peaks - top), axis=0, keepdims=True)
            sent[0, i : i + 1, :] = top + jnp.log(total) * LOG2E
        landed[0, me] = sent[0]
        share(sent.at[0], landed.at[0], send_sem.at[0], recv_sem.at[0])
        for i in range(count):
            part = pl.ds((first + i) * LANES, LANES)
            sent[1, i : i + 1, :] = jnp.sum(pick_lanes[part, :].T, axis=0, keepdims=True)
        landed[1, me] = sent[1]
        share(sent.at[1], landed.at[1], send_sem.at[1], recv_sem.at[1])

    others = pl.ds(0, n - 1)

    def agree(first, count, sent, landed, recv_sem):
        arrived = landed.at[0, others]
        pltpu.make_async_copy(arrived, arrived, recv_sem.at[0]).wait()
        norms = landed[0]
        top = jnp.max(norms, axis=0)
        norm = top + jnp.log(jnp.sum(jnp.exp2(norms - top[None]), axis=0)) * LOG2E
        at_label = jnp.exp2(sent[1] - norm) - 1.0
        for i in range(count):
            part = pl.ds((first + i) * LANES, LANES)
            norm_lanes[part, :] = jnp.broadcast_to(norm[i : i + 1, :], (LANES, LANES)).T
            hit_lanes[part, :] = jnp.broadcast_to(at_label[i : i + 1, :], (LANES, LANES)).T
        return norm

    def finish(step, first, count, norm, landed, send_sem, recv_sem):
        arrived = landed.at[1, others]
        pltpu.make_async_copy(arrived, arrived, recv_sem.at[1]).wait()
        loss = (norm - jnp.sum(landed[1], axis=0)) * LN2
        for i in range(count):
            columns = slice((first + i) * LANES, (first + i + 1) * LANES)
            losses_ref[step : step + 1, columns] = loss[i : i + 1, :]
        for kind in range(2):
            done = landed.at[kind, others]
            pltpu.make_async_copy(done, done, send_sem.at[kind]).wait()

    reset()

    @pl.loop(0, chunks)
    def _(c):
        for h in range(per):
            piece = c * per + h
            arrived = pl.ds(0, (n - 1) * features)
            pltpu.make_async_copy(
                incoming.at[piece, arrived], incoming.at[piece, arrived], in_sem.at[piece]
            ).wait()
            columns = slice(h * narrow, (h + 1) * narrow)

            @pl.loop(0, tiles)
            def _(i):
                here = pl.ds(pl.multiple_of(i * ROW_TILE, ROW_TILE), ROW_TILE)
                logits[c, here, columns] = (
                    jnp.dot(examples[here, :], incoming[piece], preferred_element_type=jnp.float32)
                    * LOG2E
                )

                @pl.loop(0, ROW_TILE // SUB, unroll=2)
                def _(u):
                    spot = pl.ds(pl.multiple_of(i * ROW_TILE + u * SUB, SUB), SUB)
                    collect(spot, piece * narrow, logits[c, spot, columns])

    publish(0, slabs, first_send, first_recv, first_out, first_in)
    first_norm = agree(0, slabs, first_send, first_recv, first_in)
    reset()

    @pl.loop(0, rows // SUB, unroll=4)
    def _(u):
        residual(0, pl.ds(pl.multiple_of(u * SUB, SUB), SUB), False)

    half = slabs // HALVES
    half_tiles = tiles // HALVES
    share_rows = rows // half_tiles
    for h in range(HALVES):
        for c in range(chunks):
            for i in range(half_tiles):
                here = pl.ds((h * half_tiles + i) * ROW_TILE, ROW_TILE)
                change = jnp.dot(gram[here, :], total_ref[c], preferred_element_type=jnp.float32)
                if h == 0 and c + 1 < chunks:
                    residual(c + 1, pl.ds(i * share_rows, share_rows), False)
                block = logits[c, here, :] - change
                logits[c, here, :] = block
                collect(here, c * width, block)
        publish(
            h * half, half, later_send.at[h], later_recv.at[h], later_out.at[h], later_in.at[h]
        )

    finish(0, 0, slabs, first_norm, first_recv, first_out, first_in)
    later_norms = []
    for h in range(HALVES):
        later_norms.append(agree(h * half, half, later_send.at[h], later_recv.at[h], later_in.at[h]))

        @pl.loop(0, rows // HALVES // SUB, unroll=2)
        def _(u):
            spot = pl.ds(pl.multiple_of(h * (rows // HALVES) + u * SUB, SUB), SUB)
            for c in range(chunks):
                residual(c, spot, True)

    for h in range(HALVES):
        finish(1, h * half, half, later_norms[h], later_recv.at[h], later_out.at[h], later_in.at[h])

    pltpu.make_async_copy(examples.at[peers], examples.at[peers], emb_out).wait()

    @pl.loop(0, pieces)
    def _(c):
        sent = pl.ds(0, n - 1)
        pltpu.make_async_copy(outgoing.at[c, sent], outgoing.at[c, sent], out_sem.at[c]).wait()


def update_kernel(rate, turned_ref, total_ref, losses_in, out_ref, losses_ref, held, out_sem):
    chunks, model_width, width = held.shape
    losses_ref[...] = losses_in[...]
    copies = []
    for c in range(chunks):
        for i in range(model_width // ROW_TILE):
            here = pl.ds(i * ROW_TILE, ROW_TILE)
            held[c, here, :] = -rate * jnp.dot(
                turned_ref[here, :], total_ref[c], preferred_element_type=jnp.float32
            )
            copies.append(
                pltpu.make_async_copy(
                    held.at[c, here],
                    out_ref.at[here, pl.ds(c * width, width)],
                    out_sem.at[c, i],
                )
            )
            copies[-1].start()
    for copy in copies:
        copy.wait()


def fused(embeddings, weights, labels):
    cls_n, row_n = lax.axis_size("cls"), lax.axis_size("row")
    n = cls_n * row_n
    shard_rows, model_width = embeddings.shape
    rows = shard_rows * row_n
    features = weights.shape[0]
    class_count = weights.shape[1] // n
    width = max(w for w in (128, 256, 384, 512) if class_count % w == 0)
    narrow = 256 if width % 256 == 0 else LANES
    chunks = class_count // width
    pieces = class_count // narrow
    rate = learn_rate / rows
    slabs = rows // LANES
    half = slabs // HALVES
    vmem = pl.BlockSpec(memory_space=pltpu.VMEM)
    hbm = pl.BlockSpec(memory_space=pltpu.HBM)
    dma = pltpu.SemaphoreType.DMA
    lanes = pltpu.VMEM((rows, LANES), jnp.float32)
    operands = (embeddings, weights, labels.reshape(slabs, LANES))
    total, turned, losses = pl.pallas_call(
        functools.partial(exchange_kernel, cls_n, row_n, rate),
        out_shape=(
            jax.ShapeDtypeStruct((chunks, rows, width), jnp.bfloat16),
            jax.ShapeDtypeStruct((model_width, rows), jnp.bfloat16),
            jax.ShapeDtypeStruct((STEPS, rows), jnp.float32),
        ),
        in_specs=[hbm, hbm, hbm],
        out_specs=(vmem, vmem, vmem),
        scratch_shapes=[
            pltpu.VMEM((2, n, features, narrow), jnp.float32),
            pltpu.VMEM((pieces, n, features, narrow), jnp.bfloat16),
            pltpu.VMEM((pieces, n * features, narrow), jnp.bfloat16),
            pltpu.VMEM((rows, LANES), jnp.int32),
            pltpu.VMEM((chunks, rows, width), jnp.float32),
            pltpu.VMEM((rows, rows), jnp.bfloat16),
            pltpu.VMEM((rows, model_width), jnp.bfloat16),
            pltpu.VMEM((shard_rows, model_width), jnp.float32),
            pltpu.VMEM((shard_rows, model_width), jnp.bfloat16),
            pltpu.VMEM((slabs, LANES), jnp.int32),
            lanes,
            lanes,
            lanes,
            lanes,
            lanes,
            pltpu.VMEM((2, slabs, LANES), jnp.float32),
            pltpu.VMEM((2, n, slabs, LANES), jnp.float32),
            pltpu.VMEM((HALVES, 2, half, LANES), jnp.float32),
            pltpu.VMEM((HALVES, 2, n, half, LANES), jnp.float32),
            dma((2,)),
            dma((2,)),
            dma((pieces,)),
            dma((pieces,)),
            dma,
            dma,
            dma((2,)),
            dma((2,)),
            dma((HALVES, 2)),
            dma((HALVES, 2)),
        ],
        compiler_params=pltpu.CompilerParams(
            collective_id=0, has_side_effects=True, vmem_limit_bytes=KERNEL_VMEM
        ),
    )(*(pltpu.with_memory_space_constraint(x, pltpu.HBM) for x in operands))
    update, losses = pl.pallas_call(
        functools.partial(update_kernel, rate),
        out_shape=(
            jax.ShapeDtypeStruct((model_width, class_count), jnp.float32),
            jax.ShapeDtypeStruct((STEPS, rows), jnp.float32),
        ),
        in_specs=[vmem, vmem, vmem],
        out_specs=(hbm, vmem),
        scratch_shapes=[
            pltpu.VMEM((chunks, model_width, width), jnp.float32),
            dma((chunks, model_width // ROW_TILE)),
        ],
        compiler_params=pltpu.CompilerParams(vmem_limit_bytes=UPDATE_VMEM),
    )(turned, total, losses)
    return update, losses


def shards(embeddings, weights, labels):
    if STEPS == 2 and weights.shape[0] % 16 == 0:
        return fused(embeddings, weights, labels)
    peer_count = lax.axis_size(("cls", "row"))
    examples = lax.all_gather(embeddings.astype(jnp.bfloat16), "row", axis=0, tiled=True)
    row_count = examples.shape[0]
    feature_rows = weights.shape[0]
    class_count = weights.shape[1] // peer_count
    offset = lax.axis_index(("cls", "row")) * class_count
    columns = lax.broadcasted_iota(jnp.int32, (1, class_count), 1) + offset
    label_hit = columns == labels[:, None]
    pieces = weights.astype(jnp.bfloat16).reshape(feature_rows, peer_count, class_count)
    block_weights = lax.all_to_all(
        pieces.transpose(1, 0, 2), ("cls", "row"), split_axis=0, concat_axis=0, tiled=True
    )
    flat_weights = block_weights.reshape(peer_count * feature_rows, class_count)
    first_logits = jnp.dot(examples, flat_weights, preferred_element_type=jnp.float32)
    rate = learn_rate / row_count
    gram = lax.dot_general(
        examples, examples, (((1,), (1,)), ((), ())), preferred_element_type=jnp.float32
    ).astype(jnp.bfloat16)
    total = None
    loss_rows = []
    for step_index in range(STEPS):
        logits = first_logits
        if step_index > 0:
            logits = logits - rate * jnp.dot(gram, total, preferred_element_type=jnp.float32)
        local_peak = jnp.max(logits, axis=1)
        local_total = jnp.sum(jnp.exp(logits - local_peak[:, None]), axis=1)
        local_picked = jnp.sum(jnp.where(label_hit, logits, 0.0), axis=1)
        stats = lax.all_gather(
            jnp.stack([local_peak, local_total, local_picked]), ("cls", "row"), axis=0
        )
        row_peak = jnp.max(stats[:, 0], axis=0)
        row_total = jnp.sum(stats[:, 1] * jnp.exp(stats[:, 0] - row_peak[None, :]), axis=0)
        picked = jnp.sum(stats[:, 2], axis=0)
        log_norm = row_peak + jnp.log(row_total)
        loss_rows.append(log_norm - picked)
        onehot = jnp.where(label_hit, 1.0, 0.0)
        residual = jnp.exp(logits - log_norm[:, None]) - onehot
        if total is not None:
            residual = residual + total.astype(jnp.float32)
        total = residual.astype(jnp.bfloat16)
    update = lax.dot_general(
        examples, total, (((0,), (0,)), ((), ())), preferred_element_type=jnp.float32
    )
    return (-rate * update, jnp.stack(loss_rows))


def solution(mesh):
    placed = (P("row", None), P(("cls", "row"), None), P())
    return jax.shard_map(
        shards,
        mesh=mesh,
        in_specs=placed,
        out_specs=(P(None, ("cls", "row")), P()),
        check_vma=False,
    )
```

time: 175 us -> 156 us (0.89)
  Pallas kernels: 174 us -> 154 us
    pallas_call x1, Pallas kernels: 158 us -> 147 us  [fused(): pl.pallas_call(functools.partial(exchange_kernel, cls_n, row_n, rate), ou...]
    pallas_call x1, Pallas kernels: 16.1 us -> 7.16 us  [fused(): pl.pallas_call(functools.partial(update_kernel, rate), out_shape=(jax.Sha...]
where the time goes in v1:
time: 156 us; the launch traced here: 155 us
  Pallas kernels  154 us (99%)
    pallas_call x1, Pallas kernels, fused(): pl.pallas_call(functools.partial(exchange_kernel, cls_n, row_n, rate), ou...  147 us
    pallas_call x1, Pallas kernels, fused(): pl.pallas_call(functools.partial(update_kernel, rate), out_shape=(jax.Sha...  7.16 us

profile of v1, /device:TPU:0, one launch (start us, length us, event | category | flops | bytes accessed | tf_op | source)
XLA Modules:
  0.0 155.2 jit_solution(4681371444478574801)
XLA Ops:
  0.6 147.2 %shard_map.50 = (bf16[5,1024,512]{2,1,0:T(8,128)(2,1)S(1)}, bf16[1024,1024]{1,0:T(8,128)(2,1)S(1)}, f32[2,1024]{1,0:T(2,128)S(1)}) custom-call(f32[256,1024]{1,0:T(8,128)} %emb_hbm.1, f32[32,81920]{1,0:T(8,128)} %weights_ref.1, s32[8,128]{1,0:T(8,128)} %bitcast.1), custom_call_target="tpu_custom_call" | custom-call | tf_op jit(solution)/shard_map/pallas_call | solution.py:371
  147.8 7.2 %shard_map.51 = (f32[1024,2560]{1,0:T(8,128)}, f32[2,1024]{1,0:T(2,128)}) custom-call(bf16[1024,1024]{1,0:T(8,128)(2,1)S(1)} %get-tuple-element.5.turned_ref, bf16[5,1024,512]{2,1,0:T(8,128)(2,1)S(1)} %get-tuple-element.6.total_ref, f32[2,1024]{1,0:T(2,128)S(1)} %get-tuple-element.7.losses_in), custom_call_target="tpu_custom_call" | custom-call | tf_op jit(solution)/shard_map/pallas_call | solution.py:415

commit v2 on v1

--- a/solution.py
+++ b/solution.py
@@ -16,7 +16,6 @@
 LANES = 128
 ROW_TILE = 256
 SUB = 32
-HALVES = 2
 LOG2E = 1.4426950408889634
 LN2 = 0.6931471805599453
 KERNEL_VMEM = 40 * 1024 * 1024
@@ -30,8 +29,9 @@
     emb_hbm,
     weights_ref,
     labels_hbm,
-    total_ref,
-    turned_ref,
+    update_ref,
+    late_ref,
+    late_turned,
     losses_ref,
     stage,
     outgoing,
@@ -40,6 +40,7 @@
     logits,
     gram,
     examples,
+    early_turned,
     emb_ref,
     emb_bf,
     labels_ref,
@@ -74,6 +75,9 @@
     tiles = rows // ROW_TILE
     groups = width // LANES
     slabs = rows // LANES
+    half_rows = rows // 2
+    half = slabs // 2
+    total_ref = incoming
 
     def place(p):
         return (lax.div(p, row_n), lax.rem(p, row_n))
@@ -113,13 +117,15 @@
         slot = lax.rem(c, 2)
         pltpu.make_async_copy(stage.at[slot], stage.at[slot], load_sem.at[slot]).wait()
         spot = pl.ds(pl.multiple_of(me * features, features), features)
+        chunk = lax.div(c, per)
+        columns = pl.ds(pl.multiple_of(lax.rem(c, per) * narrow, narrow), narrow)
 
         def send(j):
             p = lax.rem(me + j + n // 2, n)
             outgoing[c, p] = stage[slot, p].astype(jnp.bfloat16)
             pltpu.make_async_remote_copy(
                 src_ref=outgoing.at[c, p],
-                dst_ref=incoming.at[c, spot],
+                dst_ref=incoming.at[chunk, spot, columns],
                 send_sem=out_sem.at[c],
                 recv_sem=in_sem.at[c],
                 device_id=place(p),
@@ -127,7 +133,7 @@
             ).start()
 
         pl.loop(0, n // 2)(send)
-        incoming[c, spot] = stage[slot, me].astype(jnp.bfloat16)
+        incoming[chunk, spot, columns] = stage[slot, me].astype(jnp.bfloat16)
         pl.loop(n // 2 + 1, n)(send)
 
         @pl.when(c == 0)
@@ -165,7 +171,14 @@
             preferred_element_type=jnp.float32,
         )
         gram[here, :] = (product * (rate * LOG2E)).astype(jnp.bfloat16)
-        turned_ref[:, here] = examples[here, :].astype(jnp.float32).T.astype(jnp.bfloat16)
+
+    for i in range(tiles):
+        here = pl.ds(i * ROW_TILE, ROW_TILE)
+        turned = examples[here, :].astype(jnp.float32).T.astype(jnp.bfloat16)
+        if i * ROW_TILE < half_rows:
+            early_turned[:, here] = turned
+        else:
+            late_turned[:, pl.ds(i * ROW_TILE - half_rows, ROW_TILE)] = turned
 
     def reset():
         peak_lanes[...] = jnp.full_like(peak_lanes, -3.0e38)
@@ -191,7 +204,7 @@
         sum_lanes[spot, :] = total
         pick_lanes[spot, :] = picked
 
-    def residual(c, spot, earlier):
+    def residual(c, spot, earlier=False, to=None, to_spot=None):
         norm = norm_lanes[spot, :]
         at_label = hit_lanes[spot, :]
         for q, hit in enumerate(hits(spot, c * width, groups)):
@@ -200,7 +213,10 @@
             value = jnp.where(hit, at_label, jnp.exp2(part - norm)).astype(jnp.bfloat16)
             if earlier:
                 value = value + total_ref[c, spot, columns]
-            total_ref[c, spot, columns] = value
+            if to is None:
+                total_ref[c, spot, columns] = value
+            else:
+                to[c, to_spot, columns] = value
 
     def share(src, dst, send_sem, recv_sem):
         @pl.loop(1, n)
@@ -214,46 +230,40 @@
                 device_id_type=MESH,
             ).start()
 
-    def publish(first, count, sent, landed, send_sem, recv_sem):
+    def log_sums(first, count, sent):
         for i in range(count):
             part = pl.ds((first + i) * LANES, LANES)
             peaks = peak_lanes[part, :].T
             top = jnp.max(peaks, axis=0, keepdims=True)
             total = jnp.sum(sum_lanes[part, :].T * jnp.exp2(peaks - top), axis=0, keepdims=True)
-            sent[0, i : i + 1, :] = top + jnp.log(total) * LOG2E
-        landed[0, me] = sent[0]
-        share(sent.at[0], landed.at[0], send_sem.at[0], recv_sem.at[0])
+            sent[i : i + 1, :] = top + jnp.log(total) * LOG2E
+
+    def label_sums(first, count, sent, at):
         for i in range(count):
             part = pl.ds((first + i) * LANES, LANES)
-            sent[1, i : i + 1, :] = jnp.sum(pick_lanes[part, :].T, axis=0, keepdims=True)
-        landed[1, me] = sent[1]
-        share(sent.at[1], landed.at[1], send_sem.at[1], recv_sem.at[1])
+            sent[at + i : at + i + 1, :] = jnp.sum(pick_lanes[part, :].T, axis=0, keepdims=True)
 
     others = pl.ds(0, n - 1)
 
-    def agree(first, count, sent, landed, recv_sem):
-        arrived = landed.at[0, others]
-        pltpu.make_async_copy(arrived, arrived, recv_sem.at[0]).wait()
-        norms = landed[0]
+    def wait(landed, sem):
+        pltpu.make_async_copy(landed.at[others], landed.at[others], sem).wait()
+
+    def agree(first, norms, picked):
+        count = picked.shape[0]
         top = jnp.max(norms, axis=0)
         norm = top + jnp.log(jnp.sum(jnp.exp2(norms - top[None]), axis=0)) * LOG2E
-        at_label = jnp.exp2(sent[1] - norm) - 1.0
+        at_label = jnp.exp2(picked - norm) - 1.0
         for i in range(count):
             part = pl.ds((first + i) * LANES, LANES)
             norm_lanes[part, :] = jnp.broadcast_to(norm[i : i + 1, :], (LANES, LANES)).T
             hit_lanes[part, :] = jnp.broadcast_to(at_label[i : i + 1, :], (LANES, LANES)).T
         return norm
 
-    def finish(step, first, count, norm, landed, send_sem, recv_sem):
-        arrived = landed.at[1, others]
-        pltpu.make_async_copy(arrived, arrived, recv_sem.at[1]).wait()
-        loss = (norm - jnp.sum(landed[1], axis=0)) * LN2
-        for i in range(count):
+    def record(step, first, norm, picks):
+        loss = (norm - jnp.sum(picks, axis=0)) * LN2
+        for i in range(loss.shape[0]):
             columns = slice((first + i) * LANES, (first + i + 1) * LANES)
             losses_ref[step : step + 1, columns] = loss[i : i + 1, :]
-        for kind in range(2):
-            done = landed.at[kind, others]
-            pltpu.make_async_copy(done, done, send_sem.at[kind]).wait()
 
     reset()
 
@@ -262,16 +272,19 @@
         for h in range(per):
             piece = c * per + h
             arrived = pl.ds(0, (n - 1) * features)
-            pltpu.make_async_copy(
-                incoming.at[piece, arrived], incoming.at[piece, arrived], in_sem.at[piece]
-            ).wait()
-            columns = slice(h * narrow, (h + 1) * narrow)
+            columns = pl.ds(h * narrow, narrow)
+            landed = incoming.at[c, arrived, columns]
+            pltpu.make_async_copy(landed, landed, in_sem.at[piece]).wait()
 
             @pl.loop(0, tiles)
             def _(i):
                 here = pl.ds(pl.multiple_of(i * ROW_TILE, ROW_TILE), ROW_TILE)
                 logits[c, here, columns] = (
-                    jnp.dot(examples[here, :], incoming[piece], preferred_element_type=jnp.float32)
+                    jnp.dot(
+                        examples[here, :],
+                        incoming[c, :, columns],
+                        preferred_element_type=jnp.float32,
+                    )
                     * LOG2E
                 )
 
@@ -280,45 +293,66 @@
                     spot = pl.ds(pl.multiple_of(i * ROW_TILE + u * SUB, SUB), SUB)
                     collect(spot, piece * narrow, logits[c, spot, columns])
 
-    publish(0, slabs, first_send, first_recv, first_out, first_in)
-    first_norm = agree(0, slabs, first_send, first_recv, first_in)
+    log_sums(0, slabs, first_send.at[0])
+    first_recv[0, me] = first_send[0]
+    share(first_send.at[0], first_recv.at[0], first_out.at[0], first_in.at[0])
+    label_sums(0, slabs, first_send.at[1], 0)
+    first_recv[1, me] = first_send[1]
+    share(first_send.at[1], first_recv.at[1], first_out.at[1], first_in.at[1])
     reset()
+    wait(first_recv.at[0], first_in.at[0])
+    first_norm = agree(0, first_recv[0], first_send[1])
 
     @pl.loop(0, rows // SUB, unroll=4)
     def _(u):
-        residual(0, pl.ds(pl.multiple_of(u * SUB, SUB), SUB), False)
-
-    half = slabs // HALVES
-    half_tiles = tiles // HALVES
-    share_rows = rows // half_tiles
-    for h in range(HALVES):
+        residual(0, pl.ds(pl.multiple_of(u * SUB, SUB), SUB))
+
+    for h in range(2):
+        here = pl.ds(h * half_rows, half_rows)
         for c in range(chunks):
-            for i in range(half_tiles):
-                here = pl.ds((h * half_tiles + i) * ROW_TILE, ROW_TILE)
-                change = jnp.dot(gram[here, :], total_ref[c], preferred_element_type=jnp.float32)
-                if h == 0 and c + 1 < chunks:
-                    residual(c + 1, pl.ds(i * share_rows, share_rows), False)
-                block = logits[c, here, :] - change
-                logits[c, here, :] = block
-                collect(here, c * width, block)
-        publish(
-            h * half, half, later_send.at[h], later_recv.at[h], later_out.at[h], later_in.at[h]
-        )
-
-    finish(0, 0, slabs, first_norm, first_recv, first_out, first_in)
-    later_norms = []
-    for h in range(HALVES):
-        later_norms.append(agree(h * half, half, later_send.at[h], later_recv.at[h], later_in.at[h]))
-
-        @pl.loop(0, rows // HALVES // SUB, unroll=2)
-        def _(u):
-            spot = pl.ds(pl.multiple_of(h * (rows // HALVES) + u * SUB, SUB), SUB)
-            for c in range(chunks):
-                residual(c, spot, True)
-
-    for h in range(HALVES):
-        finish(1, h * half, half, later_norms[h], later_recv.at[h], later_out.at[h], later_in.at[h])
-
+            change = jnp.dot(gram[here, :], total_ref[c], preferred_element_type=jnp.float32)
+            if h == 0 and c + 1 < chunks:
+                residual(c + 1, pl.ds(0, rows))
+            block = logits[c, here, :] - change
+            logits[c, here, :] = block
+            collect(here, c * width, block)
+        log_sums(h * half, half, later_send.at[h])
+        label_sums(h * half, half, later_send.at[h], half)
+        later_recv[h, me] = later_send[h]
+        share(later_send.at[h], later_recv.at[h], later_out.at[h], later_in.at[h])
+
+    wait(later_recv.at[0], later_in.at[0])
+    early_norm = agree(0, later_recv[0, :, :half, :], later_send[0, half:, :])
+
+    @pl.loop(0, half_rows // SUB, unroll=2)
+    def _(u):
+        spot = pl.ds(pl.multiple_of(u * SUB, SUB), SUB)
+        for c in range(chunks):
+            residual(c, spot, True)
+
+    for c in range(chunks):
+        for i in range(update_ref.shape[1] // ROW_TILE):
+            here = pl.ds(i * ROW_TILE, ROW_TILE)
+            update_ref[c, here, :] = -rate * jnp.dot(
+                early_turned[here, :], total_ref[c, :half_rows, :], preferred_element_type=jnp.float32
+            )
+
+    wait(later_recv.at[1], later_in.at[1])
+    late_norm = agree(half, later_recv[1, :, :half, :], later_send[1, half:, :])
+
+    @pl.loop(0, half_rows // SUB, unroll=2)
+    def _(u):
+        spot = pl.ds(pl.multiple_of(half_rows + u * SUB, SUB), SUB)
+        for c in range(chunks):
+            residual(c, spot, True, late_ref, pl.ds(pl.multiple_of(u * SUB, SUB), SUB))
+
+    wait(first_recv.at[1], first_in.at[1])
+    record(0, 0, first_norm, first_recv[1])
+    record(1, 0, early_norm, later_recv[0, :, half:, :])
+    record(1, half, late_norm, later_recv[1, :, half:, :])
+    for k in range(2):
+        wait(first_recv.at[k], first_out.at[k])
+        wait(later_recv.at[k], later_out.at[k])
     pltpu.make_async_copy(examples.at[peers], examples.at[peers], emb_out).wait()
 
     @pl.loop(0, pieces)
@@ -327,14 +361,16 @@
         pltpu.make_async_copy(outgoing.at[c, sent], outgoing.at[c, sent], out_sem.at[c]).wait()
 
 
-def update_kernel(rate, turned_ref, total_ref, losses_in, out_ref, losses_ref, held, out_sem):
+def update_kernel(
+    rate, early_ref, turned_ref, total_ref, losses_in, out_ref, losses_ref, held, out_sem
+):
     chunks, model_width, width = held.shape
     losses_ref[...] = losses_in[...]
     copies = []
     for c in range(chunks):
         for i in range(model_width // ROW_TILE):
             here = pl.ds(i * ROW_TILE, ROW_TILE)
-            held[c, here, :] = -rate * jnp.dot(
+            held[c, here, :] = early_ref[c, here, :] - rate * jnp.dot(
                 turned_ref[here, :], total_ref[c], preferred_element_type=jnp.float32
             )
             copies.append(
@@ -362,29 +398,31 @@
     pieces = class_count // narrow
     rate = learn_rate / rows
     slabs = rows // LANES
-    half = slabs // HALVES
+    half_rows = rows // 2
     vmem = pl.BlockSpec(memory_space=pltpu.VMEM)
     hbm = pl.BlockSpec(memory_space=pltpu.HBM)
     dma = pltpu.SemaphoreType.DMA
     lanes = pltpu.VMEM((rows, LANES), jnp.float32)
     operands = (embeddings, weights, labels.reshape(slabs, LANES))
-    total, turned, losses = pl.pallas_call(
+    early, late, turned, losses = pl.pallas_call(
         functools.partial(exchange_kernel, cls_n, row_n, rate),
         out_shape=(
-            jax.ShapeDtypeStruct((chunks, rows, width), jnp.bfloat16),
-            jax.ShapeDtypeStruct((model_width, rows), jnp.bfloat16),
+            jax.ShapeDtypeStruct((chunks, model_width, width), jnp.float32),
+            jax.ShapeDtypeStruct((chunks, half_rows, width), jnp.bfloat16),
+            jax.ShapeDtypeStruct((model_width, half_rows), jnp.bfloat16),
             jax.ShapeDtypeStruct((STEPS, rows), jnp.float32),
         ),
         in_specs=[hbm, hbm, hbm],
-        out_specs=(vmem, vmem, vmem),
+        out_specs=(vmem, vmem, vmem, vmem),
         scratch_shapes=[
             pltpu.VMEM((2, n, features, narrow), jnp.float32),
             pltpu.VMEM((pieces, n, features, narrow), jnp.bfloat16),
-            pltpu.VMEM((pieces, n * features, narrow), jnp.bfloat16),
+            pltpu.VMEM((chunks, n * features, width), jnp.bfloat16),
             pltpu.VMEM((rows, LANES), jnp.int32),
             pltpu.VMEM((chunks, rows, width), jnp.float32),
             pltpu.VMEM((rows, rows), jnp.bfloat16),
             pltpu.VMEM((rows, model_width), jnp.bfloat16),
+            pltpu.VMEM((model_width, half_rows), jnp.bfloat16),
             pltpu.VMEM((shard_rows, model_width), jnp.float32),
             pltpu.VMEM((shard_rows, model_width), jnp.bfloat16),
             pltpu.VMEM((slabs, LANES), jnp.int32),
@@ -395,8 +433,8 @@
             lanes,
             pltpu.VMEM((2, slabs, LANES), jnp.float32),
             pltpu.VMEM((2, n, slabs, LANES), jnp.float32),
-            pltpu.VMEM((HALVES, 2, half, LANES), jnp.float32),
-            pltpu.VMEM((HALVES, 2, n, half, LANES), jnp.float32),
+            pltpu.VMEM((2, slabs, LANES), jnp.float32),
+            pltpu.VMEM((2, n, slabs, LANES), jnp.float32),
             dma((2,)),
             dma((2,)),
             dma((pieces,)),
@@ -405,8 +443,8 @@
             dma,
             dma((2,)),
             dma((2,)),
-            dma((HALVES, 2)),
-            dma((HALVES, 2)),
+            dma((2,)),
+            dma((2,)),
         ],
         compiler_params=pltpu.CompilerParams(
             collective_id=0, has_side_effects=True, vmem_limit_bytes=KERNEL_VMEM
@@ -418,19 +456,21 @@
             jax.ShapeDtypeStruct((model_width, class_count), jnp.float32),
             jax.ShapeDtypeStruct((STEPS, rows), jnp.float32),
         ),
-        in_specs=[vmem, vmem, vmem],
+        in_specs=[vmem, vmem, vmem, vmem],
         out_specs=(hbm, vmem),
         scratch_shapes=[
             pltpu.VMEM((chunks, model_width, width), jnp.float32),
             dma((chunks, model_width // ROW_TILE)),
         ],
         compiler_params=pltpu.CompilerParams(vmem_limit_bytes=UPDATE_VMEM),
-    )(turned, total, losses)
+    )(early, turned, late, losses)
     return update, losses
 
 
 def shards(embeddings, weights, labels):
-    if STEPS == 2 and weights.shape[0] % 16 == 0:
+    rows = embeddings.shape[0] * lax.axis_size("row")
+    square = rows == embeddings.shape[1]
+    if STEPS == 2 and square and weights.shape[0] % 16 == 0:
         return fused(embeddings, weights, labels)
     peer_count = lax.axis_size(("cls", "row"))
     examples = lax.all_gather(embeddings.astype(jnp.bfloat16), "row", axis=0, tiled=True)

time: 156 us -> 153 us (0.981)
  Pallas kernels: 154 us -> 151 us
    pallas_call x1, Pallas kernels: 7.16 us -> 4.98 us  [fused(): pl.pallas_call(functools.partial(update_kernel, rate), out_shape=(jax.Sha...]
where the time goes in v2:
time: 153 us; the launch traced here: 152 us
  Pallas kernels  151 us (99%)
    pallas_call x1, Pallas kernels, fused(): pl.pallas_call(functools.partial(exchange_kernel, cls_n, row_n, rate), ou...  146 us
    pallas_call x1, Pallas kernels, fused(): pl.pallas_call(functools.partial(update_kernel, rate), out_shape=(jax.Sha...  4.98 us

profile of v2, /device:TPU:0, one launch (start us, length us, event | category | flops | bytes accessed | tf_op | source)
XLA Modules:
  0.0 152.2 jit_solution(7164775822743296078)
XLA Ops:
  0.6 146.4 %shard_map.50 = (f32[5,1024,512]{2,1,0:T(8,128)S(1)}, bf16[5,512,512]{2,1,0:T(8,128)(2,1)S(1)}, bf16[1024,512]{1,0:T(8,128)(2,1)S(1)}, f32[2,1024]{1,0:T(2,128)S(1)}) custom-call(f32[256,1024]{1,0:T(8,128)} %emb_hbm.1, f32[32,81920]{1,0:T(8,128)} %weights_ref.1, s32[8,128]{1,0:T(8,128)} %bitcast.1), custom_call_target="tpu_custom_call" | custom-call | tf_op jit(solution)/shard_map/pallas_call | solution.py:407
  147.1 5.0 %shard_map.51 = (f32[1024,2560]{1,0:T(8,128)}, f32[2,1024]{1,0:T(2,128)}) custom-call(f32[5,1024,512]{2,1,0:T(8,128)S(1)} %get-tuple-element.6.early_ref, bf16[1024,512]{1,0:T(8,128)(2,1)S(1)} %get-tuple-element.7.turned_ref, bf16[5,512,512]{2,1,0:T(8,128)(2,1)S(1)} %get-tuple-element.8.total_ref, f32[2,1024]{1,0:T(2,128)S(1)} %get-tuple-element.9.losses_in), custom_call_target="tpu_custom_call" | custom-call | tf_op jit(solution)/shard_map/pallas_call | solution.py:453

commit v3 on v2

--- a/solution.py
+++ b/solution.py
@@ -204,23 +204,17 @@
         sum_lanes[spot, :] = total
         pick_lanes[spot, :] = picked
 
-    def residual(c, spot, earlier=False, to=None, to_spot=None):
+    def residual(c, spot, to, to_spot):
         norm = norm_lanes[spot, :]
         at_label = hit_lanes[spot, :]
         for q, hit in enumerate(hits(spot, c * width, groups)):
             columns = slice(q * LANES, (q + 1) * LANES)
             part = logits[c, spot, columns]
             value = jnp.where(hit, at_label, jnp.exp2(part - norm)).astype(jnp.bfloat16)
-            if earlier:
-                value = value + total_ref[c, spot, columns]
-            if to is None:
-                total_ref[c, spot, columns] = value
-            else:
-                to[c, to_spot, columns] = value
+            to[c, to_spot, columns] = value + total_ref[c, spot, columns]
 
     def share(src, dst, send_sem, recv_sem):
-        @pl.loop(1, n)
-        def _(k):
+        for k in range(1, n):
             pltpu.make_async_remote_copy(
                 src_ref=src,
                 dst_ref=dst.at[me],
@@ -248,16 +242,32 @@
     def wait(landed, sem):
         pltpu.make_async_copy(landed.at[others], landed.at[others], sem).wait()
 
-    def agree(first, norms, picked):
+    def agree(first, norms, picked, local=None):
         count = picked.shape[0]
         top = jnp.max(norms, axis=0)
         norm = top + jnp.log(jnp.sum(jnp.exp2(norms - top[None]), axis=0)) * LOG2E
         at_label = jnp.exp2(picked - norm) - 1.0
+        factor = norm if local is None else jnp.exp2(local - norm)
         for i in range(count):
             part = pl.ds((first + i) * LANES, LANES)
-            norm_lanes[part, :] = jnp.broadcast_to(norm[i : i + 1, :], (LANES, LANES)).T
+            norm_lanes[part, :] = jnp.broadcast_to(factor[i : i + 1, :], (LANES, LANES)).T
             hit_lanes[part, :] = jnp.broadcast_to(at_label[i : i + 1, :], (LANES, LANES)).T
         return norm
+
+    def relative(c, spot):
+        local = norm_lanes[spot, :]
+        for q, hit in enumerate(hits(spot, c * width, groups)):
+            columns = slice(q * LANES, (q + 1) * LANES)
+            value = jnp.exp2(logits[c, spot, columns] - local)
+            total_ref[c, spot, columns] = jnp.where(hit, -1.0, value).astype(jnp.bfloat16)
+
+    def rescale(c, spot):
+        factor = norm_lanes[spot, :].astype(jnp.bfloat16)
+        at_label = hit_lanes[spot, :].astype(jnp.bfloat16)
+        for q in range(groups):
+            columns = slice(q * LANES, (q + 1) * LANES)
+            value = total_ref[c, spot, columns]
+            total_ref[c, spot, columns] = jnp.where(value < 0, at_label, value * factor)
 
     def record(step, first, norm, picks):
         loss = (norm - jnp.sum(picks, axis=0)) * LN2
@@ -300,19 +310,25 @@
     first_recv[1, me] = first_send[1]
     share(first_send.at[1], first_recv.at[1], first_out.at[1], first_in.at[1])
     reset()
+    for i in range(slabs):
+        local = jnp.broadcast_to(first_send[0, i : i + 1, :], (LANES, LANES))
+        norm_lanes[pl.ds(i * LANES, LANES), :] = local.T
+
+    @pl.loop(0, rows // SUB, unroll=2)
+    def _(u):
+        for c in range(chunks):
+            relative(c, pl.ds(pl.multiple_of(u * SUB, SUB), SUB))
+
     wait(first_recv.at[0], first_in.at[0])
-    first_norm = agree(0, first_recv[0], first_send[1])
-
-    @pl.loop(0, rows // SUB, unroll=4)
-    def _(u):
-        residual(0, pl.ds(pl.multiple_of(u * SUB, SUB), SUB))
+    first_norm = agree(0, first_recv[0], first_send[1], first_send[0])
+    rescale(0, pl.ds(0, rows))
 
     for h in range(2):
         here = pl.ds(h * half_rows, half_rows)
         for c in range(chunks):
             change = jnp.dot(gram[here, :], total_ref[c], preferred_element_type=jnp.float32)
             if h == 0 and c + 1 < chunks:
-                residual(c + 1, pl.ds(0, rows))
+                rescale(c + 1, pl.ds(0, rows))
             block = logits[c, here, :] - change
             logits[c, here, :] = block
             collect(here, c * width, block)
@@ -328,7 +344,7 @@
     def _(u):
         spot = pl.ds(pl.multiple_of(u * SUB, SUB), SUB)
         for c in range(chunks):
-            residual(c, spot, True)
+            residual(c, spot, total_ref, spot)
 
     for c in range(chunks):
         for i in range(update_ref.shape[1] // ROW_TILE):
@@ -344,7 +360,7 @@
     def _(u):
         spot = pl.ds(pl.multiple_of(half_rows + u * SUB, SUB), SUB)
         for c in range(chunks):
-            residual(c, spot, True, late_ref, pl.ds(pl.multiple_of(u * SUB, SUB), SUB))
+            residual(c, spot, late_ref, pl.ds(pl.multiple_of(u * SUB, SUB), SUB))
 
     wait(first_recv.at[1], first_in.at[1])
     record(0, 0, first_norm, first_recv[1])

time: 153 us -> 152 us (level)
  no operation moved by 1% of the time
where the time goes in v3:
time: 152 us
  Pallas kernels  151 us (99%)
    pallas_call x1, Pallas kernels, fused(): pl.pallas_call(functools.partial(exchange_kernel, cls_n, row_n, rate), ou...  146 us
    pallas_call x1, Pallas kernels, fused(): pl.pallas_call(functools.partial(update_kernel, rate), out_shape=(jax.Sha...  4.98 us

profile of v3, /device:TPU:0, one launch (start us, length us, event | category | flops | bytes accessed | tf_op | source)
XLA Modules:
  0.0 151.7 jit_solution(7175714451931461429)
XLA Ops:
  0.6 145.9 %shard_map.50 = (f32[5,1024,512]{2,1,0:T(8,128)S(1)}, bf16[5,512,512]{2,1,0:T(8,128)(2,1)S(1)}, bf16[1024,512]{1,0:T(8,128)(2,1)S(1)}, f32[2,1024]{1,0:T(2,128)S(1)}) custom-call(f32[256,1024]{1,0:T(8,128)} %emb_hbm.1, f32[32,81920]{1,0:T(8,128)} %weights_ref.1, s32[8,128]{1,0:T(8,128)} %bitcast.1), custom_call_target="tpu_custom_call" | custom-call | tf_op jit(solution)/shard_map/pallas_call | solution.py:423
  146.5 5.0 %shard_map.51 = (f32[1024,2560]{1,0:T(8,128)}, f32[2,1024]{1,0:T(2,128)}) custom-call(f32[5,1024,512]{2,1,0:T(8,128)S(1)} %get-tuple-element.6.early_ref, bf16[1024,512]{1,0:T(8,128)(2,1)S(1)} %get-tuple-element.7.turned_ref, bf16[5,512,512]{2,1,0:T(8,128)(2,1)S(1)} %get-tuple-element.8.total_ref, f32[2,1024]{1,0:T(2,128)S(1)} %get-tuple-element.9.losses_in), custom_call_target="tpu_custom_call" | custom-call | tf_op jit(solution)/shard_map/pallas_call | solution.py:469

commit v4 on v3

--- a/solution.py
+++ b/solution.py
@@ -214,7 +214,8 @@
             to[c, to_spot, columns] = value + total_ref[c, spot, columns]
 
     def share(src, dst, send_sem, recv_sem):
-        for k in range(1, n):
+        @pl.loop(1, n)
+        def _(k):
             pltpu.make_async_remote_copy(
                 src_ref=src,
                 dst_ref=dst.at[me],

time: 152 us -> 152 us (level)
  no operation moved by 1% of the time
where the time goes in v4:
time: 152 us; the launch traced here: 151 us
  Pallas kernels  150 us (99%)
    pallas_call x1, Pallas kernels, fused(): pl.pallas_call(functools.partial(exchange_kernel, cls_n, row_n, rate), ou...  145 us
    pallas_call x1, Pallas kernels, fused(): pl.pallas_call(functools.partial(update_kernel, rate), out_shape=(jax.Sha...  4.98 us

profile of v4, /device:TPU:0, one launch (start us, length us, event | category | flops | bytes accessed | tf_op | source)
XLA Modules:
  0.0 150.9 jit_solution(9789573469394454857)
XLA Ops:
  0.6 145.2 %shard_map.50 = (f32[5,1024,512]{2,1,0:T(8,128)S(1)}, bf16[5,512,512]{2,1,0:T(8,128)(2,1)S(1)}, bf16[1024,512]{1,0:T(8,128)(2,1)S(1)}, f32[2,1024]{1,0:T(2,128)S(1)}) custom-call(f32[256,1024]{1,0:T(8,128)} %emb_hbm.1, f32[32,81920]{1,0:T(8,128)} %weights_ref.1, s32[8,128]{1,0:T(8,128)} %bitcast.1), custom_call_target="tpu_custom_call" | custom-call | tf_op jit(solution)/shard_map/pallas_call | solution.py:424
  145.8 5.0 %shard_map.51 = (f32[1024,2560]{1,0:T(8,128)}, f32[2,1024]{1,0:T(2,128)}) custom-call(f32[5,1024,512]{2,1,0:T(8,128)S(1)} %get-tuple-element.6.early_ref, bf16[1024,512]{1,0:T(8,128)(2,1)S(1)} %get-tuple-element.7.turned_ref, bf16[5,512,512]{2,1,0:T(8,128)(2,1)S(1)} %get-tuple-element.8.total_ref, f32[2,1024]{1,0:T(2,128)S(1)} %get-tuple-element.9.losses_in), custom_call_target="tpu_custom_call" | custom-call | tf_op jit(solution)/shard_map/pallas_call | solution.py:470
